TPU v7x, 32 devices: a whole 2x2x4 slice. The times are simulated.
32 devices in a mesh: cand: 4 (over x, core), blk: 4 (over z), feat: 2 (over y).
Axes of the slice: x: 2, y: 2, z: 4, core: 2. Of those that a mesh axis runs over, the one named last changes fastest.
Arguments:
- embeddings: float32 [32768, 1024], P(('cand', 'blk'), 'feat'), may hold values from -12 to 12
- winners: int32 [32, 3], replicated, may hold values from 0 to 32767, as said below
Outputs:
- columns: float32 [32, 3, 32768], P(None, None, ('cand', 'blk'))
- gains: float32 [32, 32768], P(None, ('cand', 'blk'))
- best: float32 [32, 3], replicated
Inputs may be any that keep to these rules, and one draw needn't show every extreme that they name: winners[b,k] lies in [k * 10922, (k + 1) * 10922), so the winners of a session are distinct.
All inputs are finite; a program needn't handle non-finite values.
Results may differ from a plain program's by a relative error of at most 0.00012.
Values sent between devices are 32-bit elements; how exact they have to be, the bound alone decides.
A program may use at most 64 MiB of HBM per device.

v0:
```python
import jax
import jax.numpy as jnp
from jax import lax
from jax.sharding import PartitionSpec as P

D = 1024


def small_factor(gram_sum, norm_win):
    steps = gram_sum.shape[1]
    factor_rows = []
    radius_list = []
    for t in range(steps):
        carried = jnp.zeros_like(gram_sum[:, t, :])
        lowered = norm_win[:, t]
        for u in range(t):
            carried = carried + factor_rows[u][:, t : t + 1] * factor_rows[u]
            lowered = lowered - factor_rows[u][:, t] * factor_rows[u][:, t]
        radius = jnp.sqrt(jnp.maximum(lowered, 0.1))
        factor_rows.append((gram_sum[:, t, :] - carried) / radius[:, None])
        radius_list.append(radius)
    return (factor_rows, radius_list)


def columns_from(inner, factor_rows, radius_list):
    steps = inner.shape[1]
    finished = []
    for t in range(steps):
        carried = jnp.zeros_like(inner[:, t, :])
        for u in range(t):
            carried = carried + factor_rows[u][:, t : t + 1] * finished[u]
        finished.append((inner[:, t, :] - carried) / radius_list[t][:, None])
    return jnp.stack(finished, axis=1)


def batched_steps(embeddings, winners, positions, squared):
    rows_here = embeddings.shape[0]
    sessions = winners.shape[0]
    steps = winners.shape[1]
    chosen = winners.reshape(sessions * steps)
    onehot = (positions[None, :] == chosen[:, None]).astype(jnp.float32)
    row_part = jnp.dot(
        onehot, embeddings, precision=lax.Precision.HIGHEST, preferred_element_type=jnp.float32
    )
    norm_part = jnp.dot(
        onehot, squared, precision=lax.Precision.HIGHEST, preferred_element_type=jnp.float32
    )
    row_win, norm_win = lax.psum((row_part, norm_part), ("cand", "blk"))
    partial_value = lax.dot_general(
        row_win,
        embeddings,
        (((1,), (1,)), ((), ())),
        precision=lax.Precision.HIGHEST,
        preferred_element_type=jnp.float32,
    )
    partial_value = partial_value.reshape(sessions, steps, rows_here)
    row_set = row_win.reshape(sessions, steps, row_win.shape[1])
    gram_part = jnp.einsum("bsf,btf->bst", row_set, row_set, precision=lax.Precision.HIGHEST)
    norm_win = norm_win.reshape(sessions, steps)
    inner, gram_sum = lax.psum((partial_value, gram_part), "feat")
    factor_rows, radius_list = small_factor(gram_sum / D, norm_win)
    return columns_from(inner / D, factor_rows, radius_list)


def body(embeddings, winners):
    rows_here = embeddings.shape[0]
    sessions = winners.shape[0]
    steps = winners.shape[1]
    offset = lax.axis_index(("cand", "blk")) * rows_here
    positions = offset + jnp.arange(rows_here, dtype=jnp.int32)
    squared = lax.psum(jnp.sum(embeddings * embeddings, axis=1), "feat") / D
    columns = batched_steps(embeddings, winners, positions, squared)
    gains = jnp.broadcast_to(squared[None, :], (sessions, rows_here))
    maxima = []
    for k in range(steps):
        maxima.append(jnp.max(gains, axis=1))
        gains = gains - columns[:, k, :] * columns[:, k, :]
    best = jnp.stack([lax.pmax(top, ("cand", "blk")) for top in maxima], axis=1)
    return (columns, gains, best)


def solution(mesh):
    placed = (P(("cand", "blk"), "feat"), P())
    return jax.shard_map(
        body,
        mesh=mesh,
        in_specs=placed,
        out_specs=(P(None, None, ("cand", "blk")), P(None, ("cand", "blk")), P()),
        check_vma=False,
    )
```

profile of v0, /device:TPU:0, one launch (start us, length us, event | category | flops | bytes accessed | tf_op | source)
XLA Modules:
  0.0 234.4 jit_solution(16774206742729019312)
XLA Ops:
  7.2 0.0 all-reduce.5.cloned.1.call-start
  7.2 0.8 copy.19
  8.0 0.1 eq.16
  8.1 4.5 %fusion.1 = f32[96,512]{1,0:T(8,128)} fusion(f32[2048,512]{1,0:T(8,128)} %param.2, s32[2048]{0:T(1024)S(1)} %iota_add_fusion, s32[96]{0:T(128)S(1)} %eq.16), kind=kOutput, calls=%fused_computation.3 | convolution fusion | flops 1208156160 | bytes 4399488 | tf_op jit(solution)/shard_map/dot_general | solution.py:42
  12.6 0.0 all-reduce.5.cloned.1.call-update
  12.7 0.0 all-reduce.7.cloned.1.call-start
  12.7 2.5 %multiply_reduce_fusion = f32[2048]{0:T(1024)S(1)} fusion(f32[2048,512]{1,0:T(8,128)} %param.2), kind=kLoop, calls=%fused_computation | loop fusion | flops 2095104 | bytes 4202496 | tf_op jit(solution)/shard_map/reduce_sum | solution.py:71
  15.2 91.0 %all-reduce.5.cloned.1.call-done = f32[96,512]{1,0:T(8,128)} async-done(((f32[96,512]{1,0:T(8,128)}), f32[96,512]{1,0:T(8,128)}) %all-reduce.5.cloned.1.call-update) | async-done | bytes 196624 | tf_op jit(solution)/shard_map/psum | solution.py:48
  106.3 1.0 reshape.83
  107.3 0.8 fusion.17
  108.1 8.9 %all-reduce.1 = (f32[2048]{0:T(1024)S(1)}, f32[32,3,3]{2,1,0:T(4,128)S(1)}) all-reduce(f32[2048]{0:T(1024)S(1)} %multiply_reduce_fusion, f32[32,3,3]{2,1,0:T(4,128)S(1)} %fusion.17), channel_id=1, replica_groups=mesh['cand'=4,'blk'=4,'feat'=2] {'feat'}, use_global_device_ids=true, to_apply=%region_3.0 | all-reduce | flops 2336 | bytes 18688 | tf_op jit(solution)/shard_map/psum | solution.py:71
  117.0 0.6 fusion.14
  117.6 0.5 convolution_bitcast_fusion
  118.1 0.1 reshape.82
  118.2 0.1 copy.21
  118.3 31.0 %psum.38 = f32[32,3]{0,1:T(4,128)S(1)} all-reduce(f32[32,3]{0,1:T(4,128)S(1)} %copy.21), channel_id=1, replica_groups=mesh['cand'=4,'blk'=4,'feat'=2] {'cand','blk'}, use_global_device_ids=true, to_apply=%region_4.0 | all-reduce | flops 96 | bytes 768 | tf_op jit(solution)/shard_map/psum | solution.py:48
  149.4 0.1 copy.22
  149.5 0.1 copy.23
  149.5 6.4 %fusion.16 = f32[96,2048]{1,0:T(8,128)S(1)} fusion(f32[96,512]{1,0:T(8,128)} %all-reduce.5.cloned.1.call-done, f32[2048,512]{1,0:T(8,128)} %param.2), kind=kOutput, calls=%fused_computation.40 | convolution fusion | flops 1207959552 | bytes 5177344 | tf_op jit(solution)/shard_map/dot_general | solution.py:49
  155.9 0.3 reshape.81
  156.3 1.3 copy.20
  157.6 0.0 all-reduce.7.cloned.1.call-update
  157.7 32.0 %all-reduce.7.cloned.1.call-done = f32[32,3,2048]{2,0,1:T(8,128)} async-done(((f32[32,3,2048]{2,0,1:T(8,128)}), f32[32,3,2048]{2,0,1:T(8,128)}) %all-reduce.7.cloned.1.call-update) | async-done | bytes 786448 | tf_op jit(solution)/shard_map/psum | solution.py:60
  189.8 1.2 broadcast_multiply_fusion
  191.0 1.1 fusion.11
  192.0 0.2 subtract_divide_fusion
  192.2 0.9 pad_maximum_fusion
  193.2 0.6 broadcast.56
  193.8 33.2 %all-reduce = (f32[32,1]{0,1:T(1,128)S(1)}, f32[32,1]{0,1:T(1,128)S(1)}, f32[32,1]{0,1:T(1,128)S(1)}) all-reduce(f32[32,1]{0,1:T(1,128)S(1)} %bitcast.57, f32[32,1]{0,1:T(1,128)S(1)} %bitcast.56, f32[32,1]{0,1:T(1,128)S(1)} %broadcast.56), channel_id=1, replica_groups=mesh['cand'=4,'blk'=4,'feat'=2] {'cand','blk'}, use_global_device_ids=true, to_apply=%region_11.0 | all-reduce | flops 96 | bytes 768 | tf_op jit(solution)/shard_map/pmax | solution.py:78
  227.0 0.6 pad_maximum_fusion.1
  (8 shorter events, 0.1 us)
Async XLA Ops:
  7.2 99.1 %all-reduce.5.cloned.1.call-start = ((), (), s32[]{:S(2)}) async-start(), calls=%async_computation | async-start | bytes 393216 | tf_op jit(solution)/shard_map/psum | solution.py:48
  12.7 177.1 %all-reduce.7.cloned.1.call-start = ((), (), s32[]{:S(2)}) async-start(), calls=%async_computation.1 | async-start | bytes 1572864 | tf_op jit(solution)/shard_map/psum | solution.py:60
Sparse Core Ops, SparseCore 0:
  12.8 93.4 all-reduce.4
  157.8 31.9 all-reduce.6
where the time goes:
time: 235 us; the launch traced here: 234 us
  waiting for transfers between devices  123 us (52%)
  blocking collectives  73.1 us (31%)
  between operations  14.2 us (6%)
  matrix products  12.2 us (5%)
  other arithmetic  7.18 us (3%)
  local copies, waits for them, and re-layouts  4.57 us (2%)
    psum x1, waiting for transfers between devices, batched_steps(): row_win, norm_win = lax.psum((row_part, norm_part), ('cand', 'blk'))  91 us
    pmax x1, blocking collectives, body(): best = jnp.stack([lax.pmax(top, ('cand', 'blk')) for top in maxima], axis=1)  33.2 us
    psum x1, waiting for transfers between devices, batched_steps(): inner, gram_sum = lax.psum((partial_value, gram_part), 'feat')  32 us
    psum x1, blocking collectives, batched_steps(): row_win, norm_win = lax.psum((row_part, norm_part), ('cand', 'blk'))  31 us
    psum x1, blocking collectives, body(): squared = lax.psum(jnp.sum(embeddings * embeddings, axis=1), 'feat') / D  8.92 us
    dot_general x1, matrix products, batched_steps(): lax.dot_general(row_win, embeddings, (((1,), (1,)), ((), ())), precision=...  6.39 us
  transfers between devices with their start and end apart: 2, of which 2 were waited for; matrix products, arithmetic and copies ran while one was open for 1% of the time, Pallas kernels for 0%

commit v1 on v0

v1 whole, which is shorter than its diff:
```python
import functools
import jax
import jax.numpy as jnp
from jax import lax
from jax.experimental import pallas as pl
from jax.experimental.pallas import tpu as pltpu
from jax.sharding import PartitionSpec as P

MESH = pl.DeviceIdType.MESH
F32 = jnp.float32
LANES = 128
SUB = 8


def spans(rows_here, group, steps):
    third = rows_here * group // steps
    return [(k * third // rows_here, ((k + 1) * third - 1) // rows_here) for k in range(steps)]


def kernel(cfg, win_ref, emb_hbm, col_ref, gain_ref, best_ref,
           emb, picked, slots, rows, part, inpart, gram, ingram, sq, insq, top, intop,
           load_sem, rs_send, rs_recv, ag_send, ag_recv, sq_send, sq_recv,
           gr_send, gr_recv, in_send, in_recv, top_send, top_recv):
    group, blks, feats, sessions, steps, chunk, total_width = cfg
    rows_here, width = emb_hbm.shape
    me = lax.axis_index("cand") * blks + lax.axis_index("blk")
    myfeat = lax.axis_index("feat")
    lane_blocks = width // LANES
    pieces = (sessions // SUB) * lane_blocks
    offset = me * rows_here

    def peer(index):
        return {"cand": index // blks, "blk": lax.rem(index, blks)}

    def mate(d):
        return {"feat": lax.rem(myfeat + d, feats)}

    def owner(index):
        return index < pieces

    load = pltpu.make_async_copy(emb_hbm, emb, load_sem)
    load.start()
    barrier = pltpu.get_barrier_semaphore()
    for d in range(1, group):
        pl.semaphore_signal(barrier, inc=1, device_id=peer(lax.rem(me + d, group)), device_id_type=MESH)
    for d in range(1, feats):
        pl.semaphore_signal(barrier, inc=1, device_id=mate(d), device_id_type=MESH)
    load.wait()

    span = spans(rows_here, group, steps)
    for k in range(steps):
        for b in range(sessions):
            at = win_ref[b, k] - offset
            inside = jnp.logical_and(at >= 0, at < rows_here)
            safe = jnp.clip(at, 0, rows_here - 1)
            row = emb[pl.ds(safe, 1), :]
            picked[k, b : b + 1, :] = jnp.where(inside, row, jnp.zeros_like(row))
    pl.semaphore_wait(barrier, group - 1 + feats - 1)

    def tile_at(index):
        r = pl.multiple_of(index // lane_blocks * SUB, SUB)
        c = pl.multiple_of(lax.rem(index, lane_blocks) * LANES, LANES)
        return pl.ds(r, SUB), pl.ds(c, LANES)

    def scatter_copy(k, d):
        to = lax.rem(me + d, group)
        at = lax.rem(to, pieces)
        r, c = tile_at(at)
        return pltpu.make_async_remote_copy(
            src_ref=picked.at[k, r, c],
            dst_ref=slots.at[k, me - span[k][0]],
            send_sem=rs_send.at[k, d - 1],
            recv_sem=rs_recv.at[k, me - span[k][0]],
            device_id=peer(to),
            device_id_type=MESH,
        )

    def contributes(k):
        return jnp.logical_and(me >= span[k][0], me <= span[k][1])

    for k in range(steps):
        @pl.when(contributes(k))
        def _(k=k):
            for d in range(1, group):
                @pl.when(owner(lax.rem(me + d, group)))
                def _(d=d):
                    scatter_copy(k, d).start()

            @pl.when(owner(me))
            def _():
                r, c = tile_at(lax.rem(me, pieces))
                slots[k, me - span[k][0]] = picked[k, r, c]

    for s in range(0, rows_here, 512):
        folded = jnp.zeros((512, LANES), F32)
        for l in range(lane_blocks):
            x = emb[s : s + 512, l * LANES : (l + 1) * LANES]
            folded = folded + x * x
        sq[:, s : s + 512] = jnp.sum(folded.T, axis=0, keepdims=True)

    def sq_copy(d):
        return pltpu.make_async_remote_copy(
            src_ref=sq, dst_ref=insq.at[d - 1], send_sem=sq_send.at[d - 1], recv_sem=sq_recv.at[d - 1],
            device_id=mate(d), device_id_type=MESH)

    def gather_copy(d, sender):
        r, c = tile_at(lax.rem(sender, pieces))
        return pltpu.make_async_remote_copy(
            src_ref=rows.at[:, r, c], dst_ref=rows.at[:, r, c],
            send_sem=ag_send.at[d - 1], recv_sem=ag_recv.at[d - 1],
            device_id=peer(lax.rem(me + d, group)), device_id_type=MESH)

    @pl.when(owner(me))
    def _():
        r, c = tile_at(lax.rem(me, pieces))
        for k in range(steps):
            for who in range(span[k][0], span[k][1] + 1):
                @pl.when(me != who)
                def _(k=k, who=who):
                    slot = slots.at[k, who - span[k][0]]
                    pltpu.make_async_remote_copy(
                        src_ref=slot, dst_ref=slot,
                        send_sem=rs_send.at[k, 0], recv_sem=rs_recv.at[k, who - span[k][0]],
                        device_id=peer(who), device_id_type=MESH).wait_recv()
        for k in range(steps):
            acc = slots[k, 0]
            for s in range(1, span[k][1] - span[k][0] + 1):
                acc = acc + slots[k, s]
            rows[k, r, c] = acc
        for d in range(1, group):
            gather_copy(d, me).start()

    for d in range(1, feats):
        sq_copy(d).start()

    for d in range(1, group):
        sender = lax.rem(me + group - d, group)
        @pl.when(owner(sender))
        def _(d=d, sender=sender):
            gather_copy(d, sender).wait_recv()

    lane = lax.broadcasted_iota(jnp.int32, (sessions, LANES), 1)
    pairs = [(t, u) for t in range(steps) for u in range(t + 1)]
    packed = jnp.zeros((sessions, LANES), F32)
    for i, (t, u) in enumerate(pairs):
        value = jnp.sum(rows[t] * rows[u], axis=1, keepdims=True)
        packed = jnp.where(lane == i, value, packed)
    gram[...] = packed

    def gram_copy(d):
        return pltpu.make_async_remote_copy(
            src_ref=gram, dst_ref=ingram.at[d - 1], send_sem=gr_send.at[d - 1], recv_sem=gr_recv.at[d - 1],
            device_id=mate(d), device_id_type=MESH)

    def part_copy(n, d):
        where = pl.ds(n * chunk, chunk)
        return pltpu.make_async_remote_copy(
            src_ref=part.at[:, where], dst_ref=inpart.at[d - 1, :, where],
            send_sem=in_send.at[n, d - 1], recv_sem=in_recv.at[n, d - 1],
            device_id=mate(d), device_id_type=MESH)

    chunks = rows_here // chunk
    lhs = rows[...].reshape(steps * sessions, width)
    for n in range(chunks):
        part[:, n * chunk : (n + 1) * chunk] = lax.dot_general(
            lhs, emb[n * chunk : (n + 1) * chunk, :], (((1,), (1,)), ((), ())),
            precision=lax.Precision.HIGHEST, preferred_element_type=F32)
        if n == 0:
            for d in range(1, feats):
                gram_copy(d).start()
        for d in range(1, feats):
            part_copy(n, d).start()

    for d in range(1, feats):
        sq_copy(d).wait_recv()
        gram_copy(d).wait_recv()
    both = gram[...]
    norms = sq[...]
    for d in range(1, feats):
        both = both + ingram[d - 1]
        norms = norms + insq[d - 1]
    both = both / total_width
    norms = norms / total_width
    factor = {}
    radius = []
    for t in range(steps):
        at = {u: both[:, i : i + 1] for i, (v, u) in enumerate(pairs) if v == t}
        lowered = at[t]
        for u in range(t):
            value = at[u]
            for w in range(u):
                value = value - factor[u, w] * factor[t, w]
            value = value / radius[u]
            factor[t, u] = value
            lowered = lowered - value * value
        radius.append(jnp.sqrt(jnp.maximum(lowered, 0.1)))

    tops = [None] * steps
    for n in range(chunks):
        for d in range(1, feats):
            part_copy(n, d).wait_recv()
        where = slice(n * chunk, (n + 1) * chunk)
        gains = jnp.broadcast_to(norms[:, where], (sessions, chunk))
        finished = []
        for t in range(steps):
            folded = gains[:, :LANES]
            for l in range(1, chunk // LANES):
                folded = jnp.maximum(folded, gains[:, l * LANES : (l + 1) * LANES])
            tops[t] = folded if tops[t] is None else jnp.maximum(tops[t], folded)
            inner = part[t * sessions : (t + 1) * sessions, where]
            for d in range(1, feats):
                inner = inner + inpart[d - 1, t * sessions : (t + 1) * sessions, where]
            inner = inner / total_width
            carried = jnp.zeros_like(inner)
            for u in range(t):
                carried = carried + factor[t, u] * finished[u]
            column = (inner - carried) / radius[t]
            finished.append(column)
            col_ref[t, :, where] = column
            gains = gains - column * column
        gain_ref[:, where] = gains

    pad = -(steps * sessions) % LANES
    stacked = jnp.concatenate(tops + ([jnp.zeros((pad, LANES), F32)] if pad else []), axis=0)
    top[...] = jnp.max(stacked.T, axis=0, keepdims=True)

    def top_copy(d):
        return pltpu.make_async_remote_copy(
            src_ref=top, dst_ref=intop.at[d - 1], send_sem=top_send.at[d - 1], recv_sem=top_recv.at[d - 1],
            device_id=peer(lax.rem(me + d, group)), device_id_type=MESH)

    for d in range(1, group):
        top_copy(d).start()

    for k in range(steps):
        @pl.when(contributes(k))
        def _(k=k):
            for d in range(1, group):
                @pl.when(owner(lax.rem(me + d, group)))
                def _(d=d):
                    scatter_copy(k, d).wait_send()

    @pl.when(owner(me))
    def _():
        for d in range(1, group):
            gather_copy(d, me).wait_send()

    for d in range(1, feats):
        sq_copy(d).wait_send()
        gram_copy(d).wait_send()
        for n in range(chunks):
            part_copy(n, d).wait_send()

    for d in range(1, group):
        top_copy(d).wait_recv()
    best = top[...]
    for d in range(1, group):
        best = jnp.maximum(best, intop[d - 1])
    best_ref[...] = best
    for d in range(1, group):
        top_copy(d).wait_send()


def body(cands, blks, feats, embeddings, winners):
    rows_here, width = embeddings.shape
    sessions, steps = winners.shape
    group = cands * blks
    chunk = min(256, rows_here)
    chunks = rows_here // chunk
    wide = max(b - a + 1 for a, b in spans(rows_here, group, steps))
    lanes = -(-steps * sessions // LANES) * LANES
    dma = pltpu.SemaphoreType.DMA
    cfg = (group, blks, feats, sessions, steps, chunk, width * feats)
    vmem = pl.BlockSpec(memory_space=pltpu.VMEM)
    columns, gains, best = pl.pallas_call(
        functools.partial(kernel, cfg),
        out_shape=(
            jax.ShapeDtypeStruct((steps, sessions, rows_here), F32),
            jax.ShapeDtypeStruct((sessions, rows_here), F32),
            jax.ShapeDtypeStruct((1, lanes), F32),
        ),
        in_specs=[pl.BlockSpec(memory_space=pltpu.SMEM), pl.BlockSpec(memory_space=pl.ANY)],
        out_specs=(vmem, vmem, vmem),
        scratch_shapes=[
            pltpu.VMEM((rows_here, width), F32),
            pltpu.VMEM((steps, sessions, width), F32),
            pltpu.VMEM((steps, wide, SUB, LANES), F32),
            pltpu.VMEM((steps, sessions, width), F32),
            pltpu.VMEM((steps * sessions, rows_here), F32),
            pltpu.VMEM((feats - 1, steps * sessions, rows_here), F32),
            pltpu.VMEM((sessions, LANES), F32),
            pltpu.VMEM((feats - 1, sessions, LANES), F32),
            pltpu.VMEM((1, rows_here), F32),
            pltpu.VMEM((feats - 1, 1, rows_here), F32),
            pltpu.VMEM((1, lanes), F32),
            pltpu.VMEM((group - 1, 1, lanes), F32),
            dma,
            dma((steps, group - 1)),
            dma((steps, wide)),
            dma((group - 1,)),
            dma((group - 1,)),
            dma((feats - 1,)),
            dma((feats - 1,)),
            dma((feats - 1,)),
            dma((feats - 1,)),
            dma((chunks, feats - 1)),
            dma((chunks, feats - 1)),
            dma((group - 1,)),
            dma((group - 1,)),
        ],
        compiler_params=pltpu.CompilerParams(collective_id=0, has_side_effects=True),
    )(winners, embeddings)
    best = best[0, : steps * sessions].reshape(steps, sessions).T
    return columns.transpose(1, 0, 2), gains, best


def solution(mesh):
    shape = mesh.shape
    return jax.shard_map(
        functools.partial(body, shape["cand"], shape["blk"], shape["feat"]),
        mesh=mesh,
        in_specs=(P(("cand", "blk"), "feat"), P()),
        out_specs=(P(None, None, ("cand", "blk")), P(None, ("cand", "blk")), P()),
        check_vma=False,
    )
```

time: 235 us -> 52.1 us (0.22)
  waiting for transfers between devices: 123 us -> 0 us
  blocking collectives: 73.1 us -> 0 us
  Pallas kernels: 0 us -> 44.7 us
  between operations: 14.2 us -> 0.64 us
  matrix products: 12.2 us -> 0 us
  other arithmetic: 7.18 us -> 0 us
    psum x2 -> x0, waiting for transfers between devices: 123 us -> none  [the longest x1 91 us: batched_steps(): row_win, norm_win = lax.psum((row_part, norm_part), ('cand', 'blk'))]
    pallas_call x0 -> x1, Pallas kernels: none -> 44.7 us  [body(): pl.pallas_call(functools.partial(kernel, cfg), out_shape=(jax.ShapeDtypeS...]
    psum x2 -> x0, blocking collectives: 39.9 us -> none  [the longest x1 31 us: batched_steps(): row_win, norm_win = lax.psum((row_part, norm_part), ('cand', 'blk'))]
    pmax x1 -> x0, blocking collectives: 33.2 us -> none  [body(): best = jnp.stack([lax.pmax(top, ('cand', 'blk')) for top in maxima], axis=1)]
    dot_general x4 -> x0, matrix products: 12.2 us -> none  [the longest x1 6.39 us: batched_steps(): lax.dot_general(row_win, embeddings, (((1,), (1,)), ((), ())), precision=...]
    unnamed x1 -> x3, local copies, waits for them, and re-layouts: 0.76 us -> 5.1 us
    reshape x5 -> x0, local copies, waits for them, and re-layouts: 2.88 us -> none  [the longest x2 1.68 us: batched_steps(): partial_value = partial_value.reshape(sessions, steps, rows_here)]
    reduce_sum x1 -> x0, other arithmetic: 2.54 us -> none  [body(): squared = lax.psum(jnp.sum(embeddings * embeddings, axis=1), 'feat') / D]
  transfers between devices with their start and end apart: 2 -> 0, of which waited for: 2 -> 0; matrix products, arithmetic and copies ran while one was open for 1% -> 0% of each run, Pallas kernels for 0% -> 0%
where the time goes in v1:
time: 52.1 us; the launch traced here: 51.8 us
  Pallas kernels  44.7 us (86%)
  local copies, waits for them, and re-layouts  6.45 us (12%)
  between operations  0.64 us (1%)
    pallas_call x1, Pallas kernels, body(): pl.pallas_call(functools.partial(kernel, cfg), out_shape=(jax.ShapeDtypeS...  44.7 us
    unnamed x3, local copies, waits for them, and re-layouts  5.1 us

profile of v1, /device:TPU:0, one launch (start us, length us, event | category | flops | bytes accessed | tf_op | source)
XLA Modules:
  0.0 51.8 jit_solution(11614040666442444913)
XLA Ops:
  0.6 1.4 %copy.5.win_ref = s32[32,3]{1,0:T(8,128)} copy(s32[32,3]{0,1:T(4,128)} %param.3) | data formatting | bytes 768 | tf_op args[1]
  2.0 44.7 %shard_map.49 = (f32[3,32,2048]{2,1,0:T(8,128)}, f32[32,2048]{1,0:T(8,128)}, f32[1,128]{1,0:T(1,128)}) custom-call(s32[32,3]{1,0:T(8,128)} %copy.5.win_ref, f32[2048,512]{1,0:T(8,128)} %emb_hbm.1), custom_call_target="tpu_custom_call" | custom-call | tf_op jit(solution)/shard_map/pallas_call | solution.py:275
  46.7 0.7 %slice_reduce_fusion = f32[96]{0:T(128)S(1)} fusion(f32[1,128]{1,0:T(1,128)} %get-tuple-element.8), kind=kLoop, calls=%fused_computation | loop fusion | bytes 768 | tf_op jit(solution)/shard_map/slice | solution.py:313
  47.4 0.7 %reshape_squeeze.3 = f32[3,32]{1,0:T(4,128)} reshape(f32[96]{0:T(128)S(1)} %slice_reduce_fusion) | data formatting | bytes 768 | tf_op jit(solution)/shard_map/reshape;squeeze | solution.py:313
  48.1 2.1 %copy.8 = f32[32,3,2048]{2,0,1:T(8,128)} copy(f32[32,3,2048]{2,0,1:T(8,128)} %bitcast.2) | data formatting | bytes 1572864
  50.1 1.7 %copy.9 = f32[32,2048]{1,0:T(8,128)} copy(f32[32,2048]{1,0:T(8,128)} %get-tuple-element.13) | data formatting | bytes 524288

commit v2 on v1

--- a/solution.py
+++ b/solution.py
@@ -17,9 +17,9 @@
     return [(k * third // rows_here, ((k + 1) * third - 1) // rows_here) for k in range(steps)]
 
 
-def kernel(cfg, win_ref, emb_hbm, col_ref, gain_ref, best_ref,
-           emb, picked, slots, rows, part, inpart, gram, ingram, sq, insq, top, intop,
-           load_sem, rs_send, rs_recv, ag_send, ag_recv, sq_send, sq_recv,
+def kernel(cfg, win_hbm, emb_hbm, col_hbm, gain_hbm, best_ref,
+           win_ref, col_ref, gain_ref, emb, picked, slots, rows, part, inpart, gram, ingram, sq, insq, top, intop,
+           win_sem, load_sem, out_sem, rs_send, rs_recv, ag_send, ag_recv, sq_send, sq_recv,
            gr_send, gr_recv, in_send, in_recv, top_send, top_recv):
     group, blks, feats, sessions, steps, chunk, total_width = cfg
     rows_here, width = emb_hbm.shape
@@ -40,17 +40,20 @@
 
     load = pltpu.make_async_copy(emb_hbm, emb, load_sem)
     load.start()
+    win_load = pltpu.make_async_copy(win_hbm, win_ref, win_sem)
+    win_load.start()
     barrier = pltpu.get_barrier_semaphore()
     for d in range(1, group):
         pl.semaphore_signal(barrier, inc=1, device_id=peer(lax.rem(me + d, group)), device_id_type=MESH)
     for d in range(1, feats):
         pl.semaphore_signal(barrier, inc=1, device_id=mate(d), device_id_type=MESH)
+    win_load.wait()
     load.wait()
 
     span = spans(rows_here, group, steps)
     for k in range(steps):
         for b in range(sessions):
-            at = win_ref[b, k] - offset
+            at = win_ref[k, b] - offset
             inside = jnp.logical_and(at >= 0, at < rows_here)
             safe = jnp.clip(at, 0, rows_here - 1)
             row = emb[pl.ds(safe, 1), :]
@@ -90,13 +93,6 @@
             def _():
                 r, c = tile_at(lax.rem(me, pieces))
                 slots[k, me - span[k][0]] = picked[k, r, c]
-
-    for s in range(0, rows_here, 512):
-        folded = jnp.zeros((512, LANES), F32)
-        for l in range(lane_blocks):
-            x = emb[s : s + 512, l * LANES : (l + 1) * LANES]
-            folded = folded + x * x
-        sq[:, s : s + 512] = jnp.sum(folded.T, axis=0, keepdims=True)
 
     def sq_copy(d):
         return pltpu.make_async_remote_copy(
@@ -130,9 +126,6 @@
         for d in range(1, group):
             gather_copy(d, me).start()
 
-    for d in range(1, feats):
-        sq_copy(d).start()
-
     for d in range(1, group):
         sender = lax.rem(me + group - d, group)
         @pl.when(owner(sender))
@@ -141,11 +134,6 @@
 
     lane = lax.broadcasted_iota(jnp.int32, (sessions, LANES), 1)
     pairs = [(t, u) for t in range(steps) for u in range(t + 1)]
-    packed = jnp.zeros((sessions, LANES), F32)
-    for i, (t, u) in enumerate(pairs):
-        value = jnp.sum(rows[t] * rows[u], axis=1, keepdims=True)
-        packed = jnp.where(lane == i, value, packed)
-    gram[...] = packed
 
     def gram_copy(d):
         return pltpu.make_async_remote_copy(
@@ -153,23 +141,37 @@
             device_id=mate(d), device_id_type=MESH)
 
     def part_copy(n, d):
-        where = pl.ds(n * chunk, chunk)
-        return pltpu.make_async_remote_copy(
-            src_ref=part.at[:, where], dst_ref=inpart.at[d - 1, :, where],
+        return pltpu.make_async_remote_copy(
+            src_ref=part.at[n], dst_ref=inpart.at[d - 1, n],
             send_sem=in_send.at[n, d - 1], recv_sem=in_recv.at[n, d - 1],
             device_id=mate(d), device_id_type=MESH)
 
     chunks = rows_here // chunk
     lhs = rows[...].reshape(steps * sessions, width)
     for n in range(chunks):
-        part[:, n * chunk : (n + 1) * chunk] = lax.dot_general(
+        part[n] = lax.dot_general(
             lhs, emb[n * chunk : (n + 1) * chunk, :], (((1,), (1,)), ((), ())),
             precision=lax.Precision.HIGHEST, preferred_element_type=F32)
+        for d in range(1, feats):
+            part_copy(n, d).start()
         if n == 0:
+            packed = jnp.zeros((sessions, LANES), F32)
+            for i, (t, u) in enumerate(pairs):
+                value = jnp.sum(rows[t] * rows[u], axis=1, keepdims=True)
+                packed = jnp.where(lane == i, value, packed)
+            gram[...] = packed
             for d in range(1, feats):
                 gram_copy(d).start()
-        for d in range(1, feats):
-            part_copy(n, d).start()
+
+    for s in range(0, rows_here, 512):
+        folded = jnp.zeros((512, LANES), F32)
+        for l in range(lane_blocks):
+            x = emb[s : s + 512, l * LANES : (l + 1) * LANES]
+            folded = folded + x * x
+        sq[:, s : s + 512] = jnp.sum(folded.T, axis=0, keepdims=True)
+
+    for d in range(1, feats):
+        sq_copy(d).start()
 
     for d in range(1, feats):
         sq_copy(d).wait_recv()
@@ -195,6 +197,13 @@
             lowered = lowered - value * value
         radius.append(jnp.sqrt(jnp.maximum(lowered, 0.1)))
 
+    def out_copies(n):
+        where = pl.ds(n * chunk, chunk)
+        return (
+            pltpu.make_async_copy(col_ref.at[:, :, where], col_hbm.at[:, :, where], out_sem.at[0, n]),
+            pltpu.make_async_copy(gain_ref.at[:, where], gain_hbm.at[:, where], out_sem.at[1, n]),
+        )
+
     tops = [None] * steps
     for n in range(chunks):
         for d in range(1, feats):
@@ -207,9 +216,9 @@
             for l in range(1, chunk // LANES):
                 folded = jnp.maximum(folded, gains[:, l * LANES : (l + 1) * LANES])
             tops[t] = folded if tops[t] is None else jnp.maximum(tops[t], folded)
-            inner = part[t * sessions : (t + 1) * sessions, where]
+            inner = part[n, t * sessions : (t + 1) * sessions, :]
             for d in range(1, feats):
-                inner = inner + inpart[d - 1, t * sessions : (t + 1) * sessions, where]
+                inner = inner + inpart[d - 1, n, t * sessions : (t + 1) * sessions, :]
             inner = inner / total_width
             carried = jnp.zeros_like(inner)
             for u in range(t):
@@ -219,6 +228,8 @@
             col_ref[t, :, where] = column
             gains = gains - column * column
         gain_ref[:, where] = gains
+        for copy in out_copies(n):
+            copy.start()
 
     pad = -(steps * sessions) % LANES
     stacked = jnp.concatenate(tops + ([jnp.zeros((pad, LANES), F32)] if pad else []), axis=0)
@@ -231,6 +242,10 @@
 
     for d in range(1, group):
         top_copy(d).start()
+
+    for n in range(chunks):
+        for copy in out_copies(n):
+            copy.wait()
 
     for k in range(steps):
         @pl.when(contributes(k))
@@ -259,6 +274,18 @@
     best_ref[...] = best
     for d in range(1, group):
         top_copy(d).wait_send()
+
+
+def deliver(col_in, gain_in, best_in, col_out, gain_out, best_out, col_sem, gain_sem):
+    col_copy = pltpu.make_async_copy(col_in, col_out, col_sem)
+    gain_copy = pltpu.make_async_copy(gain_in, gain_out, gain_sem)
+    col_copy.start()
+    gain_copy.start()
+    steps, sessions = best_out.shape
+    for k in range(steps):
+        best_out[k : k + 1, :] = best_in[:, k * sessions : (k + 1) * sessions]
+    col_copy.wait()
+    gain_copy.wait()
 
 
 def body(cands, blks, feats, embeddings, winners):
@@ -272,6 +299,7 @@
     dma = pltpu.SemaphoreType.DMA
     cfg = (group, blks, feats, sessions, steps, chunk, width * feats)
     vmem = pl.BlockSpec(memory_space=pltpu.VMEM)
+    hbm = pl.BlockSpec(memory_space=pl.ANY)
     columns, gains, best = pl.pallas_call(
         functools.partial(kernel, cfg),
         out_shape=(
@@ -279,15 +307,18 @@
             jax.ShapeDtypeStruct((sessions, rows_here), F32),
             jax.ShapeDtypeStruct((1, lanes), F32),
         ),
-        in_specs=[pl.BlockSpec(memory_space=pltpu.SMEM), pl.BlockSpec(memory_space=pl.ANY)],
-        out_specs=(vmem, vmem, vmem),
+        in_specs=[pl.BlockSpec(memory_space=pltpu.HBM)] * 2,
+        out_specs=(hbm, hbm, vmem),
         scratch_shapes=[
+            pltpu.SMEM((steps, sessions), jnp.int32),
+            pltpu.VMEM((steps, sessions, rows_here), F32),
+            pltpu.VMEM((sessions, rows_here), F32),
             pltpu.VMEM((rows_here, width), F32),
             pltpu.VMEM((steps, sessions, width), F32),
             pltpu.VMEM((steps, wide, SUB, LANES), F32),
             pltpu.VMEM((steps, sessions, width), F32),
-            pltpu.VMEM((steps * sessions, rows_here), F32),
-            pltpu.VMEM((feats - 1, steps * sessions, rows_here), F32),
+            pltpu.VMEM((chunks, steps * sessions, chunk), F32),
+            pltpu.VMEM((feats - 1, chunks, steps * sessions, chunk), F32),
             pltpu.VMEM((sessions, LANES), F32),
             pltpu.VMEM((feats - 1, sessions, LANES), F32),
             pltpu.VMEM((1, rows_here), F32),
@@ -295,6 +326,8 @@
             pltpu.VMEM((1, lanes), F32),
             pltpu.VMEM((group - 1, 1, lanes), F32),
             dma,
+            dma,
+            dma((2, chunks)),
             dma((steps, group - 1)),
             dma((steps, wide)),
             dma((group - 1,)),
@@ -308,10 +341,21 @@
             dma((group - 1,)),
             dma((group - 1,)),
         ],
-        compiler_params=pltpu.CompilerParams(collective_id=0, has_side_effects=True),
-    )(winners, embeddings)
-    best = best[0, : steps * sessions].reshape(steps, sessions).T
-    return columns.transpose(1, 0, 2), gains, best
+        compiler_params=pltpu.CompilerParams(collective_id=0, has_side_effects=True, vmem_limit_bytes=50 * 2**20),
+    )(winners.T, embeddings)
+    columns, gains, best = pl.pallas_call(
+        deliver,
+        out_shape=(
+            jax.ShapeDtypeStruct((steps, sessions, rows_here), F32),
+            jax.ShapeDtypeStruct((sessions, rows_here), F32),
+            jax.ShapeDtypeStruct((steps, sessions), F32),
+        ),
+        in_specs=[hbm, hbm, vmem],
+        out_specs=(hbm, hbm, vmem),
+        scratch_shapes=[dma, dma],
+        compiler_params=pltpu.CompilerParams(vmem_limit_bytes=4 * 2**20),
+    )(columns, gains, best)
+    return columns.transpose(1, 0, 2), gains, best.T
 
 
 def solution(mesh):

time: 52.1 us -> 47 us (0.902)
  local copies, waits for them, and re-layouts: 6.45 us -> 0.67 us
  Pallas kernels: 44.7 us -> 45.5 us
    unnamed x3 -> x2, local copies, waits for them, and re-layouts: 5.1 us -> 0.67 us
    pallas_call x0 -> x1, Pallas kernels: none -> 1.56 us  [body(): pl.pallas_call(deliver, out_shape=(jax.ShapeDtypeStruct((steps, sessions,...]
    pallas_call x1, Pallas kernels: 44.7 us -> 43.9 us  [body(): pl.pallas_call(functools.partial(kernel, cfg), out_shape=(jax.ShapeDtypeS...]
    slice x1 -> x0, local copies, waits for them, and re-layouts: 0.69 us -> none  [body(): best = best[0, :steps * sessions].reshape(steps, sessions).T]
    another operation x1 -> x0, local copies, waits for them, and re-layouts: 0.66 us -> none  [body(): best = best[0, :steps * sessions].reshape(steps, sessions).T]
where the time goes in v2:
time: 47 us; the launch traced here: 46.8 us
  Pallas kernels  45.5 us (97%)
  local copies, waits for them, and re-layouts  0.67 us (1%)
  between operations  0.65 us (1%)
    pallas_call x1, Pallas kernels, body(): pl.pallas_call(functools.partial(kernel, cfg), out_shape=(jax.ShapeDtypeS...  43.9 us
    pallas_call x1, Pallas kernels, body(): pl.pallas_call(deliver, out_shape=(jax.ShapeDtypeStruct((steps, sessions,...  1.56 us

profile of v2, /device:TPU:0, one launch (start us, length us, event | category | flops | bytes accessed | tf_op | source)
XLA Modules:
  0.0 46.8 jit_solution(4565521439026844686)
XLA Ops:
  0.6 0.0 copy-start
  0.6 0.7 %copy-done = s32[32,3]{0,1:T(4,128)S(1)} copy-done((s32[32,3]{0,1:T(4,128)S(1)}, s32[32,3]{0,1:T(4,128)}, u32[]{:S(2)}) %copy-start) | copy-done | bytes 408
  1.3 43.9 %shard_map.49 = (f32[3,32,2048]{2,1,0:T(8,128)S(1)}, f32[32,2048]{1,0:T(8,128)S(1)}, f32[1,128]{1,0:T(1,128)S(1)}) custom-call(s32[3,32]{1,0:T(4,128)S(1)} %bitcast.3, f32[2048,512]{1,0:T(8,128)} %emb_hbm.1), custom_call_target="tpu_custom_call" | custom-call | tf_op jit(solution)/shard_map/pallas_call | solution.py:303
  45.3 1.6 %shard_map.50 = (f32[3,32,2048]{2,1,0:T(8,128)}, f32[32,2048]{1,0:T(8,128)}, f32[3,32]{1,0:T(4,128)}) custom-call(f32[3,32,2048]{2,1,0:T(8,128)S(1)} %get-tuple-element.9.col_in, f32[32,2048]{1,0:T(8,128)S(1)} %get-tuple-element.10.gain_in, f32[1,128]{1,0:T(1,128)S(1)} %get-tuple-element.11.best_in), custom_call_target="tpu_custom_call" | custom-call | tf_op jit(solution)/shard_map/pallas_call | solution.py:346
Async XLA Ops:
  0.6 0.7 %copy-start = (s32[32,3]{0,1:T(4,128)S(1)}, s32[32,3]{0,1:T(4,128)}, u32[]{:S(2)}) copy-start(s32[32,3]{0,1:T(4,128)} %param.3) | copy-start | bytes 1156
